TPU v7x, 512 devices: a whole 4x4x16 slice. The times are simulated.
512 devices in a mesh: row: 64 (over z, y), col: 8 (over x, core).
Axes of the slice: x: 4, y: 4, z: 16, core: 2. Of those that a mesh axis runs over, the one named last changes fastest.
Arguments:
- right_sides: bfloat16 [1024, 128, 128], P('row'), may hold values from -6 to 6
- inverse_diag: bfloat16 [1024, 128, 128], P('row'), may hold values from -0.5 to 0.5
- off_blocks: bfloat16 [8, 1024, 6, 128, 128], P('col', 'row'), may hold values from -0.046875 to 0.046875
- owners: int32 [8, 1024, 6], P('col', 'row'), may hold values from 0 to 63, all different within a row; in each aligned block of 16 rows (0 to 15, 16 to 31, ..., all dimensions but the last counted through in order) at most 2 rows name the same one
- local_block: int32 [8, 1024, 6], P('col', 'row'), may hold values from 0 to 15
- counts: int32 [1024], P('row'), may hold values from 24 to 48
Outputs:
- solved: bfloat16 [1024, 128, 128], P('row')
Inputs may be any that keep to these rules, and one draw needn't show every extreme that they name: In the 16 block rows of one device (aligned blocks of rows of the [8, 1024] layout) a row's 6 entries are different owners, no owner is named more than 2 times, and in some blocks one owner exactly 2 times.
All inputs are finite; a program needn't handle non-finite values.
Results may differ from a plain program's by a relative error of at most 0.014.
Values may be sent and summed in bfloat16 or wider, within the bound.
A program may use at most 64 MiB of HBM per device.

v0:
```python
import jax
import jax.numpy as jnp
from jax import lax
from jax.sharding import PartitionSpec as P

ITERS = 4


def cut_along(value, dim, size):
    lengths = value.shape
    parts = value.reshape(*lengths[:dim], size, lengths[dim] // size, *lengths[dim + 1 :])
    return jnp.moveaxis(parts, dim, 0)


def sent_and_summed(value, axis, dim):
    size = lax.axis_size(axis)
    parts = lax.all_to_all(cut_along(value, dim, size), axis, 0, 0, tiled=True)
    return jnp.sum(parts.astype(jnp.float32), axis=0)


def in_order(parts, dim):
    lengths = list(parts.shape[1:])
    lengths[dim] *= parts.shape[0]
    return jnp.moveaxis(parts, 0, dim).reshape(lengths)


def copy_for_each(value, axis):
    copies = jnp.broadcast_to(value, (lax.axis_size(axis), *value.shape))
    return lax.all_to_all(copies, axis, split_axis=0, concat_axis=0, tiled=True)


def collect(value, axis, dim):
    return in_order(copy_for_each(value, axis), dim)


def apply_inverse(inverse, right):
    return jnp.einsum("bij,bjr->bir", inverse, right, preferred_element_type=jnp.float32).astype(
        jnp.bfloat16
    )


def shards(right_sides, inverse_diag, off_blocks, owners, local_block, counts):
    row_count = lax.axis_size("row")
    col_index = lax.axis_index("col")
    col_count = lax.axis_size("col")
    block_rows = counts.shape[0]
    per_group = owners.shape[2]
    owner_flat = owners.reshape(-1)
    local_flat = local_block.reshape(-1)
    slot_total = owner_flat.shape[0]
    capacity = max(2, 4 * slot_total // (3 * row_count))
    one_hot = (owner_flat[:, None] == jnp.arange(row_count, dtype=jnp.int32)[None, :]).astype(
        jnp.int32
    )
    earlier = jnp.cumsum(one_hot, axis=0) - one_hot
    bucket_rank = jnp.sum(earlier * one_hot, axis=1)
    slot_place = owner_flat * capacity + bucket_rank
    requests = jnp.zeros((row_count * capacity,), jnp.int32).at[slot_place].set(local_flat)
    wanted = lax.all_to_all(
        requests.reshape(row_count, capacity), "row", split_axis=0, concat_axis=0, tiled=True
    ).reshape(-1)
    global_slot = col_index + col_count * jnp.arange(per_group, dtype=jnp.int32)
    is_live = global_slot[None, :] < counts[:, None]
    masked = jnp.where(is_live[:, :, None, None], off_blocks[0], jnp.zeros((), jnp.bfloat16))
    solved = apply_inverse(inverse_diag, right_sides)
    share_rows = block_rows // col_count
    for iteration in range(ITERS - 1):
        outgoing = solved[wanted].reshape(row_count, capacity, solved.shape[1], solved.shape[2])
        received = lax.all_to_all(outgoing, "row", split_axis=0, concat_axis=0, tiled=True)
        columns_here = received.shape[3]
        flattened = received.reshape(row_count * capacity, received.shape[2], columns_here)
        picked = flattened[slot_place].reshape(
            block_rows, per_group, received.shape[2], columns_here
        )
        partial_value = jnp.einsum(
            "bkij,bkjr->bir", masked, picked, preferred_element_type=jnp.float32
        )
        own_sums = sent_and_summed(partial_value.astype(jnp.bfloat16), "col", 0)
        first_row = col_index * share_rows
        right_part = lax.dynamic_slice_in_dim(right_sides, first_row, share_rows, 0).astype(
            jnp.float32
        )
        inverse_part = lax.dynamic_slice_in_dim(inverse_diag, first_row, share_rows, 0)
        corrected = (right_part - own_sums).astype(jnp.bfloat16)
        solved = collect(apply_inverse(inverse_part, corrected), "col", 0)
    return solved


def solution(mesh):
    in_specs = (
        P("row", None, None),
        P("row", None, None),
        P("col", "row", None, None, None),
        P("col", "row", None),
        P("col", "row", None),
        P("row"),
    )
    out_specs = P("row", None, None)
    return jax.shard_map(shards, mesh=mesh, in_specs=in_specs, out_specs=out_specs, check_vma=False)
```

profile of v0, /device:TPU:1, one launch (start us, length us, event | category | flops | bytes accessed | tf_op | source)
XLA Modules:
  0.0 745.0 jit_solution(5896886234275230261)
XLA Ops:
  0.0 0.0 copy-start
  0.0 0.7 broadcast_multiply_fusion
  0.7 0.8 copy.14
  1.5 0.1 copy.13
  1.6 0.1 mul.35
  1.7 0.8 copy.15
  2.4 0.1 reshape.216
  2.5 0.1 eq.15
  2.6 0.1 fusion.24
  2.7 0.1 reduce_window_sum.11
  2.9 0.2 select_reduce_fusion
  3.0 0.9 scatter_custom_fusion
  3.9 0.8 all_to_all.33
  4.7 19.3 %all-to-all-start = ((s32[64,1,2]{2,1,0:T(1,128)}), s32[64,1,2]{2,1,0:T(1,128)S(1)}, u32[]{:S(2)}, u32[]{:S(2)}) async-start(s32[64,1,2]{2,1,0:T(1,128)} %bitcast.3), calls=%async_computation | async-start | bytes 65536 | tf_op jit(solution)/shard_map/all_to_all | solution.py:59
  24.0 0.0 copy-done
  24.0 1.3 convolution_convert_fusion
  25.3 12.1 %all-to-all-done = s32[64,1,2]{2,1,0:T(1,128)S(1)} async-done(((s32[64,1,2]{2,1,0:T(1,128)}), s32[64,1,2]{2,1,0:T(1,128)S(1)}, u32[]{:S(2)}, u32[]{:S(2)}) %all-to-all-start) | async-done | bytes 544 | tf_op jit(solution)/shard_map/all_to_all | solution.py:59
  37.4 0.5 broadcast.118
  37.9 0.7 reduce.3
  38.6 0.1 reshape.148
  38.8 3.1 gather_fusion
  41.8 0.0 copy-start.1
  41.8 5.8 all-to-all-start.1
  47.7 0.0 copy-done.1
  47.7 0.1 broadcast_compare_fusion
  47.7 182.4 %all-to-all-done.1 = bf16[64,2,128,128]{3,2,1,0:T(8,128)(2,1)} async-done(((bf16[64,2,128,128]{3,2,1,0:T(8,128)(2,1)}), bf16[64,2,128,128]{3,2,1,0:T(8,128)(2,1)}, u32[]{:S(2)}, u32[]{:S(2)}) %all-to-all-start.1) | async-done | bytes 4194336 | tf_op jit(solution)/shard_map/all_to_all | solution.py:69
  230.1 4.9 gather_fusion.1
  235.0 4.7 fusion.11
  239.7 12.7 %all-to-all-start.2 = ((bf16[8,2,128,128]{3,2,1,0:T(8,128)(2,1)}), bf16[8,2,128,128]{3,2,1,0:T(8,128)(2,1)S(1)}, u32[]{:S(2)}, u32[]{:S(2)}) async-start(bf16[8,2,128,128]{3,2,1,0:T(8,128)(2,1)} %bitcast.10), calls=%async_computation.2 | async-start | bytes 1048576 | tf_op jit(solution)/shard_map/all_to_all | solution.py:17
  252.4 9.3 %all-to-all-done.2 = bf16[8,2,128,128]{3,2,1,0:T(8,128)(2,1)S(1)} async-done(((bf16[8,2,128,128]{3,2,1,0:T(8,128)(2,1)}), bf16[8,2,128,128]{3,2,1,0:T(8,128)(2,1)S(1)}, u32[]{:S(2)}, u32[]{:S(2)}) %all-to-all-start.2) | async-done | bytes 524320 | tf_op jit(solution)/shard_map/all_to_all | solution.py:17
  261.8 0.1 convert_reduce_fusion.2
  261.9 1.0 convolution_convert_fusion.3
  262.9 0.1 broadcast_in_dim.20
  263.0 12.7 %all_to_all.54 = bf16[8,2,128,128]{3,2,1,0:T(8,128)(2,1)S(1)} all-to-all(bf16[8,2,128,128]{3,2,1,0:T(8,128)(2,1)S(1)} %broadcast_in_dim.20), channel_id=1, replica_groups=mesh['row'=64,'col'=8] {'col'}, dimensions={0} | all-to-all | bytes 1048576 | tf_op jit(solution)/shard_map/all_to_all | solution.py:29
  275.7 3.1 gather_fusion.2
  278.7 190.2 %all_to_all.55 = bf16[64,2,128,128]{3,2,1,0:T(8,128)(2,1)} all-to-all(bf16[64,2,128,128]{3,2,1,0:T(8,128)(2,1)} %bitcast.66), channel_id=1, replica_groups=mesh['row'=64,'col'=8] {'row'}, dimensions={0} | all-to-all | bytes 8388608 | tf_op jit(solution)/shard_map/all_to_all | solution.py:69
  469.0 4.9 gather_fusion.3
  473.9 3.9 fusion.10
  477.8 18.2 %all_to_all.56 = bf16[8,2,128,128]{3,2,1,0:T(8,128)(2,1)S(1)} all-to-all(bf16[8,2,128,128]{3,2,1,0:T(8,128)(2,1)S(1)} %bitcast.74), channel_id=1, replica_groups=mesh['row'=64,'col'=8] {'col'}, dimensions={0} | all-to-all | bytes 1048576 | tf_op jit(solution)/shard_map/all_to_all | solution.py:17
  496.0 0.1 convert_reduce_fusion.1
  496.0 1.0 convolution_convert_fusion.2
  497.1 0.1 broadcast_in_dim.21
  497.2 12.8 %all_to_all.57 = bf16[8,2,128,128]{3,2,1,0:T(8,128)(2,1)S(1)} all-to-all(bf16[8,2,128,128]{3,2,1,0:T(8,128)(2,1)S(1)} %broadcast_in_dim.21), channel_id=1, replica_groups=mesh['row'=64,'col'=8] {'col'}, dimensions={0} | all-to-all | bytes 1048576 | tf_op jit(solution)/shard_map/all_to_all | solution.py:29
  509.9 3.1 gather_fusion.4
  513.0 190.2 %all_to_all.58 = bf16[64,2,128,128]{3,2,1,0:T(8,128)(2,1)} all-to-all(bf16[64,2,128,128]{3,2,1,0:T(8,128)(2,1)} %bitcast.65), channel_id=1, replica_groups=mesh['row'=64,'col'=8] {'row'}, dimensions={0} | all-to-all | bytes 8388608 | tf_op jit(solution)/shard_map/all_to_all | solution.py:69
  703.2 4.9 gather_fusion.5
  708.1 3.9 fusion.9
  712.0 18.2 %all_to_all.59 = bf16[8,2,128,128]{3,2,1,0:T(8,128)(2,1)S(1)} all-to-all(bf16[8,2,128,128]{3,2,1,0:T(8,128)(2,1)S(1)} %bitcast.73), channel_id=1, replica_groups=mesh['row'=64,'col'=8] {'col'}, dimensions={0} | all-to-all | bytes 1048576 | tf_op jit(solution)/shard_map/all_to_all | solution.py:17
  730.2 0.1 convert_reduce_fusion
  730.3 1.0 convolution_convert_fusion.1
  731.3 0.1 broadcast_in_dim.36
  731.4 12.8 %all_to_all.60 = bf16[8,2,128,128]{3,2,1,0:T(8,128)(2,1)S(1)} all-to-all(bf16[8,2,128,128]{3,2,1,0:T(8,128)(2,1)S(1)} %broadcast_in_dim.36), channel_id=1, replica_groups=mesh['row'=64,'col'=8] {'col'}, dimensions={0} | all-to-all | bytes 1048576 | tf_op jit(solution)/shard_map/all_to_all | solution.py:29
  744.2 0.8 copy.21
  (5 shorter events, 0.0 us)
Async XLA Ops:
  0.0 24.0 %copy-start = (bf16[16,128,128]{2,1,0:T(8,128)(2,1)S(1)}, bf16[16,128,128]{2,1,0:T(8,128)(2,1)}, u32[]{:S(2)}) copy-start(bf16[16,128,128]{2,1,0:T(8,128)(2,1)} %param.7) | copy-start | bytes 1572868
  4.7 32.7 %all-to-all-start = ((s32[64,1,2]{2,1,0:T(1,128)}), s32[64,1,2]{2,1,0:T(1,128)S(1)}, u32[]{:S(2)}, u32[]{:S(2)}) async-start(s32[64,1,2]{2,1,0:T(1,128)} %bitcast.3), calls=%async_computation | async-start | bytes 65536 | tf_op jit(solution)/shard_map/all_to_all | solution.py:59
  41.8 5.8 copy-start.1
  41.8 188.3 %all-to-all-start.1 = ((bf16[64,2,128,128]{3,2,1,0:T(8,128)(2,1)}), bf16[64,2,128,128]{3,2,1,0:T(8,128)(2,1)}, u32[]{:S(2)}, u32[]{:S(2)}) async-start(bf16[64,2,128,128]{3,2,1,0:T(8,128)(2,1)} %bitcast.64), calls=%async_computation.1 | async-start | bytes 8388608 | tf_op jit(solution)/shard_map/all_to_all | solution.py:69
  239.7 22.1 %all-to-all-start.2 = ((bf16[8,2,128,128]{3,2,1,0:T(8,128)(2,1)}), bf16[8,2,128,128]{3,2,1,0:T(8,128)(2,1)S(1)}, u32[]{:S(2)}, u32[]{:S(2)}) async-start(bf16[8,2,128,128]{3,2,1,0:T(8,128)(2,1)} %bitcast.10), calls=%async_computation.2 | async-start | bytes 1048576 | tf_op jit(solution)/shard_map/all_to_all | solution.py:17
where the time goes:
time: 746 us; the launch traced here: 745 us
  blocking collectives  455 us (61%)
  waiting for transfers between devices  204 us (27%)
  starting transfers between devices  37.8 us (5%)
  local copies, waits for them, and re-layouts  29.2 us (4%)
  matrix products  16.8 us (2%)
    all_to_all x2, blocking collectives, shards(): lax.all_to_all(outgoing, 'row', split_axis=0, concat_axis=0, tiled=True)  380 us
    all_to_all x1, waiting for transfers between devices, shards(): lax.all_to_all(outgoing, 'row', split_axis=0, concat_axis=0, tiled=True)  182 us
    all_to_all x3, blocking collectives, copy_for_each(): return lax.all_to_all(copies, axis, split_axis=0, concat_axis=0, tiled=True)  38.2 us
    all_to_all x2, blocking collectives, sent_and_summed(): parts = lax.all_to_all(cut_along(value, dim, size), axis, 0, 0, tiled=True)  36.4 us
    all_to_all x1, starting transfers between devices, shards(): lax.all_to_all(requests.reshape(row_count, capacity), 'row', split_axis=0...  19.3 us
  transfers between devices with their start and end apart: 3, of which 3 were waited for; matrix products, arithmetic and copies ran while one was open for 0% of the time, Pallas kernels for 0%

commit v1 on v0

v1 whole, which is shorter than its diff:
```python
import jax
import jax.numpy as jnp
from jax import lax
from jax.experimental import pallas as pl
from jax.experimental.pallas import tpu as pltpu
from jax.sharding import PartitionSpec as P

ITERS = 4
CAP = 2


def place_kernel(rows, per_group, cols, classes_deep, owners, local, counts, blocks, placed, meta, seen, sem):
    slots = rows * per_group
    me = lax.axis_index("col")

    def clear(i, _):
        seen[i] = 0
        return 0

    lax.fori_loop(0, cols * classes_deep, clear, 0)

    def blank(i, _):
        meta[i] = -1
        return 0

    lax.fori_loop(0, cols * classes_deep * CAP, blank, 0)

    def one(s, _):
        row = s // per_group
        k = s - row * per_group
        owner = owners[s]
        again = seen[owner]
        seen[owner] = again + 1
        group = owner // cols
        where = ((owner - group * cols) * classes_deep + group) * CAP + again
        live = me + cols * k < counts[row]
        meta[where] = jnp.where(live, row * 256 + group * 16 + local[s], -1)
        pltpu.make_async_copy(blocks.at[s], placed.at[where], sem).start()
        return 0

    lax.fori_loop(0, slots, one, 0)
    pltpu.make_async_copy(blocks, placed.at[pl.ds(0, slots)], sem).wait()


def product_kernel(rows, meta, blocks, vec, out, number, listed):
    slots = blocks.shape[0]
    deep = listed.shape[1]

    def clear(i, _):
        number[i] = 0
        return 0

    lax.fori_loop(0, rows, clear, 0)

    def one(s, _):
        m = meta[s]

        @pl.when(m >= 0)
        def _():
            row = m // 256
            at = number[row]
            listed[row, at] = s * 256 + (m - row * 256)
            number[row] = at + 1

        return 0

    lax.fori_loop(0, slots, one, 0)

    for row in range(rows):
        count = number[row]

        def chunk(j, acc):
            lefts, rights = [], []
            for t in range(4):
                at = 4 * j + t
                code = listed[row, jnp.minimum(at, count - 1)]
                slot = code // 256
                left = blocks[slot]
                if t > 0:
                    left = jnp.where(at < count, left, jnp.zeros_like(left))
                lefts.append(left)
                rights.append(vec[code - slot * 256])
            for t in (0, 2):
                acc = acc + jnp.dot(
                    jnp.concatenate(lefts[t : t + 2], axis=1),
                    jnp.concatenate(rights[t : t + 2], axis=0),
                    preferred_element_type=jnp.float32,
                )
            return acc

        total = lax.fori_loop(0, (count + 3) // 4, chunk, jnp.zeros(out.shape[1:], jnp.float32))
        out[row] = total.astype(out.dtype)


def apply_inverse(inverse, right):
    return jnp.einsum("bij,bjr->bir", inverse, right, preferred_element_type=jnp.float32).astype(
        jnp.bfloat16
    )


def shards(right_sides, inverse_diag, off_blocks, owners, local_block, counts):
    row_count = lax.axis_size("row")
    col_count = lax.axis_size("col")
    col_index = lax.axis_index("col")
    rows = counts.shape[0]
    per_group = owners.shape[2]
    slots = rows * per_group
    deep = row_count // col_count
    edge = off_blocks.shape[-1]
    width = right_sides.shape[-1]
    padded = row_count * CAP
    smem = pl.BlockSpec(memory_space=pltpu.SMEM)
    vmem = pl.BlockSpec(memory_space=pltpu.VMEM)
    placed, meta = pl.pallas_call(
        lambda *refs: place_kernel(rows, per_group, col_count, deep, *refs),
        out_shape=(
            jax.ShapeDtypeStruct((padded, edge, edge), jnp.bfloat16),
            jax.ShapeDtypeStruct((padded,), jnp.int32),
        ),
        in_specs=[smem, smem, smem, pl.BlockSpec(memory_space=pl.ANY)],
        out_specs=(vmem, smem),
        scratch_shapes=[pltpu.SMEM((row_count,), jnp.int32), pltpu.SemaphoreType.DMA],
    )(
        owners.reshape(-1),
        local_block.reshape(-1),
        counts,
        off_blocks.reshape(slots, edge, edge),
    )
    here = lax.all_to_all(
        placed.reshape(col_count, padded // col_count, edge, edge), "col", 0, 0, tiled=True
    ).reshape(padded, edge, edge)
    notes = lax.all_to_all(
        meta.reshape(col_count, padded // col_count), "col", 0, 0, tiled=True
    ).reshape(-1)
    share = rows // col_count
    right_part = lax.dynamic_slice_in_dim(right_sides, col_index * share, share, 0)
    inverse_part = lax.dynamic_slice_in_dim(inverse_diag, col_index * share, share, 0)
    turn = [
        ((g * col_count + a) * col_count + c, (g * col_count + c) * col_count + a)
        for g in range(deep)
        for a in range(col_count)
        for c in range(col_count)
    ]
    mine = apply_inverse(inverse_part, right_part)
    for iteration in range(ITERS - 1):
        turned = lax.ppermute(mine, ("row", "col"), turn)
        vec = lax.all_gather(turned, "row", axis=0, tiled=True)
        partial_value = pl.pallas_call(
            lambda *refs: product_kernel(rows, *refs),
            out_shape=jax.ShapeDtypeStruct((rows, edge, width), jnp.bfloat16),
            in_specs=[smem, vmem, vmem],
            out_specs=vmem,
            scratch_shapes=[
                pltpu.SMEM((rows,), jnp.int32),
                pltpu.SMEM((rows, 64), jnp.int32),
            ],
        )(notes, here, vec)
        parts = lax.all_to_all(
            partial_value.reshape(col_count, share, edge, width), "col", 0, 0, tiled=True
        )
        sums = jnp.sum(parts.astype(jnp.float32), axis=0)
        corrected = (right_part.astype(jnp.float32) - sums).astype(jnp.bfloat16)
        mine = apply_inverse(inverse_part, corrected)
    copies = jnp.broadcast_to(mine, (col_count, *mine.shape))
    return lax.all_to_all(copies, "col", 0, 0, tiled=True).reshape(rows, edge, width)


def solution(mesh):
    in_specs = (
        P("row", None, None),
        P("row", None, None),
        P("col", "row", None, None, None),
        P("col", "row", None),
        P("col", "row", None),
        P("row"),
    )
    out_specs = P("row", None, None)
    return jax.shard_map(shards, mesh=mesh, in_specs=in_specs, out_specs=out_specs, check_vma=False)
```

time: 746 us -> 574 us (0.77)
  blocking collectives: 455 us -> 94.8 us
  waiting for transfers between devices: 204 us -> 392 us
  Pallas kernels: 0 us -> 44.8 us
  starting transfers between devices: 37.8 us -> 15.6 us
  local copies, waits for them, and re-layouts: 29.2 us -> 8.41 us
  between operations: 0.18 us -> 13.2 us
  matrix products: 16.8 us -> 4 us
    all_to_all x7 -> x5, blocking collectives: 455 us -> 94.8 us  [the longest x3 67.3 us: shards(): lax.all_to_all(partial_value.reshape(col_count, share, edge, width), 'col...]
    all_gather x0 -> x3, waiting for transfers between devices: none -> 336 us  [shards(): vec = lax.all_gather(turned, 'row', axis=0, tiled=True)]
    all_to_all x3 -> x1, waiting for transfers between devices: 204 us -> 47 us  [shards(): lax.all_to_all(placed.reshape(col_count, padded // col_count, edge, edge)...]
    pallas_call x0 -> x4, Pallas kernels: none -> 44.8 us  [the longest x3 37.9 us: shards(): pl.pallas_call(lambda *refs: product_kernel(rows, *refs), out_shape=jax.S...]
    all_to_all x3 -> x1, starting transfers between devices: 37.8 us -> 5.12 us  [shards(): lax.all_to_all(placed.reshape(col_count, padded // col_count, edge, edge)...]
    gather x6 -> x0, local copies, waits for them, and re-layouts: 23.9 us -> none  [the longest x3 14.8 us: shards(): flattened[slot_place]]
    dot_general x3 -> x0, matrix products: 12.4 us -> none  [shards(): jnp.einsum('bkij,bkjr->bir', masked, picked, preferred_element_type=jnp.f...]
    ppermute x0 -> x3, starting transfers between devices: none -> 10.4 us  [shards(): turned = lax.ppermute(mine, ('row', 'col'), turn)]
  transfers between devices with their start and end apart: 3 -> 7, of which waited for: 3 -> 7; matrix products, arithmetic and copies ran while one was open for 0% -> 1% of each run, Pallas kernels for 0% -> 1%
where the time goes in v1:
time: 574 us; the launch traced here: 573 us
  waiting for transfers between devices  392 us (68%)
  blocking collectives  94.8 us (17%)
  Pallas kernels  44.8 us (8%)
  starting transfers between devices  15.6 us (3%)
  between operations  13.2 us (2%)
  local copies, waits for them, and re-layouts  8.41 us (1%)
    all_gather x3, waiting for transfers between devices, shards(): vec = lax.all_gather(turned, 'row', axis=0, tiled=True)  336 us
    all_to_all x3, blocking collectives, shards(): lax.all_to_all(partial_value.reshape(col_count, share, edge, width), 'col...  67.3 us
    all_to_all x1, waiting for transfers between devices, shards(): lax.all_to_all(placed.reshape(col_count, padded // col_count, edge, edge)...  47 us
    pallas_call x3, Pallas kernels, shards(): pl.pallas_call(lambda *refs: product_kernel(rows, *refs), out_shape=jax.S...  37.9 us
    all_to_all x1, blocking collectives, shards(): lax.all_to_all(meta.reshape(col_count, padded // col_count), 'col', 0, 0,...  14.7 us
    all_to_all x1, blocking collectives, shards(): lax.all_to_all(copies, 'col', 0, 0, tiled=True).reshape(rows, edge, width)  12.8 us
  transfers between devices with their start and end apart: 7, of which 7 were waited for; matrix products, arithmetic and copies ran while one was open for 1% of the time, Pallas kernels for 1%

profile of v1, /device:TPU:1, one launch (start us, length us, event | category | flops | bytes accessed | tf_op | source)
XLA Modules:
  0.0 573.3 jit_solution(2317203768434341431)
XLA Ops:
  6.5 0.0 copy-start
  6.5 0.0 all-gather.4.cloned.1.call-start
  6.5 1.0 copy-done
  7.6 1.0 convolution_convert_fusion.3
  8.6 4.6 collective-permute-start
  13.2 1.9 collective-permute-done
  15.1 0.0 copy-start.1
  15.1 0.6 copy-done.1
  15.7 0.0 all-gather.4.cloned.1.call-update
  15.7 0.8 copy.11
  16.5 0.6 reshape.35.refs_0_
  17.1 0.8 copy.12
  17.9 0.6 reshape.36.refs_1_
  18.5 6.9 %shard_map.64 = (bf16[128,128,128]{2,1,0:T(8,128)(2,1)}, s32[128]{0:T(128)}) custom-call(s32[96]{0:T(128)} %reshape.35.refs_0_, s32[96]{0:T(128)} %reshape.36.refs_1_, s32[16]{0:T(128)} %refs_2_.1, bf16[96,128,128]{2,1,0:T(8,128)(2,1)} %bitcast.9), custom_call_target="tpu_custom_call" | custom-call | tf_op jit(solution)/shard_map/pallas_call | solution.py:114
  25.4 0.7 all_to_all.21
  26.1 14.7 %all_to_all.34 = s32[8,1,16]{2,1,0:T(1,128)S(1)} all-to-all(s32[8,1,16]{2,1,0:T(1,128)S(1)} %bitcast.14), channel_id=1, replica_groups=mesh['row'=64,'col'=8] {'col'}, dimensions={0} | all-to-all | bytes 1024 | tf_op jit(solution)/shard_map/all_to_all | solution.py:132
  40.8 5.1 all-to-all-start.1
  45.9 0.0 all-gather.6.cloned.1.call-start
  45.9 0.5 broadcast.3
  46.5 0.6 reduce.3
  47.1 0.6 reshape.38.refs_0_
  47.7 47.0 %all-to-all-done.1 = bf16[8,16,128,128]{3,2,1,0:T(8,128)(2,1)} async-done(((bf16[8,16,128,128]{3,2,1,0:T(8,128)(2,1)}), bf16[8,16,128,128]{3,2,1,0:T(8,128)(2,1)}, u32[]{:S(2)}, u32[]{:S(2)}) %all-to-all-start.1) | async-done | bytes 4194336 | tf_op jit(solution)/shard_map/all_to_all | solution.py:129
  94.7 67.3 %all-gather.4.cloned.1.call-done.refs_2_ = bf16[128,128,128]{2,1,0:T(8,128)(2,1)} async-done(((bf16[2,128,128]{2,1,0:T(8,128)(2,1)}), bf16[128,128,128]{2,1,0:T(8,128)(2,1)}) %all-gather.4.cloned.1.call-update) | async-done | bytes 4194320 | tf_op jit(solution)/shard_map/all_gather | solution.py:147
  162.0 12.7 %shard_map.65 = bf16[16,128,128]{2,1,0:T(8,128)(2,1)} custom-call(s32[128]{0:T(128)} %reshape.38.refs_0_, bf16[128,128,128]{2,1,0:T(8,128)(2,1)} %bitcast.3.refs_1_, bf16[128,128,128]{2,1,0:T(8,128)(2,1)} %all-gather.4.cloned.1.call-done.refs_2_), custom_call_target="tpu_custom_call" | custom-call | tf_op jit(solution)/shard_map/pallas_call | solution.py:148
  174.7 22.4 %all_to_all.35 = bf16[8,2,128,128]{3,2,1,0:T(8,128)(2,1)S(1)} all-to-all(bf16[8,2,128,128]{3,2,1,0:T(8,128)(2,1)} %bitcast.11), channel_id=1, replica_groups=mesh['row'=64,'col'=8] {'col'}, dimensions={0} | all-to-all | bytes 1048576 | tf_op jit(solution)/shard_map/all_to_all | solution.py:158
  197.1 0.1 convert_reduce_fusion.2
  197.2 1.0 convolution_convert_fusion.2
  198.2 2.9 collective-permute-start.1
  201.1 3.2 collective-permute-done.1
  204.3 0.0 copy-start.2
  204.3 0.6 copy-done.2
  204.9 0.0 all-gather.6.cloned.1.call-update
  204.9 0.0 all-gather.8.cloned.1.call-start
  205.0 134.5 %all-gather.6.cloned.1.call-done.refs_2_ = bf16[128,128,128]{2,1,0:T(8,128)(2,1)} async-done(((bf16[2,128,128]{2,1,0:T(8,128)(2,1)}), bf16[128,128,128]{2,1,0:T(8,128)(2,1)}) %all-gather.6.cloned.1.call-update) | async-done | bytes 4194320 | tf_op jit(solution)/shard_map/all_gather | solution.py:147
  339.5 12.6 %shard_map.66 = bf16[16,128,128]{2,1,0:T(8,128)(2,1)} custom-call(s32[128]{0:T(128)} %reshape.38.refs_0_, bf16[128,128,128]{2,1,0:T(8,128)(2,1)} %bitcast.3.refs_1_, bf16[128,128,128]{2,1,0:T(8,128)(2,1)} %all-gather.6.cloned.1.call-done.refs_2_), custom_call_target="tpu_custom_call" | custom-call | tf_op jit(solution)/shard_map/pallas_call | solution.py:148
  352.2 22.4 %all_to_all.36 = bf16[8,2,128,128]{3,2,1,0:T(8,128)(2,1)S(1)} all-to-all(bf16[8,2,128,128]{3,2,1,0:T(8,128)(2,1)} %bitcast.12), channel_id=1, replica_groups=mesh['row'=64,'col'=8] {'col'}, dimensions={0} | all-to-all | bytes 1048576 | tf_op jit(solution)/shard_map/all_to_all | solution.py:158
  374.6 0.1 convert_reduce_fusion.1
  374.7 1.0 convolution_convert_fusion.1
  375.7 2.9 collective-permute-start.2
  378.6 3.2 collective-permute-done.2
  381.8 0.0 copy-start.3
  381.8 0.6 copy-done.3
  382.4 0.0 all-gather.8.cloned.1.call-update
  382.4 134.6 %all-gather.8.cloned.1.call-done.refs_2_ = bf16[128,128,128]{2,1,0:T(8,128)(2,1)} async-done(((bf16[2,128,128]{2,1,0:T(8,128)(2,1)}), bf16[128,128,128]{2,1,0:T(8,128)(2,1)}) %all-gather.8.cloned.1.call-update) | async-done | bytes 4194320 | tf_op jit(solution)/shard_map/all_gather | solution.py:147
  517.0 12.6 %shard_map.67 = bf16[16,128,128]{2,1,0:T(8,128)(2,1)} custom-call(s32[128]{0:T(128)} %reshape.38.refs_0_, bf16[128,128,128]{2,1,0:T(8,128)(2,1)} %bitcast.3.refs_1_, bf16[128,128,128]{2,1,0:T(8,128)(2,1)} %all-gather.8.cloned.1.call-done.refs_2_), custom_call_target="tpu_custom_call" | custom-call | tf_op jit(solution)/shard_map/pallas_call | solution.py:148
  529.6 22.4 %all_to_all.37 = bf16[8,2,128,128]{3,2,1,0:T(8,128)(2,1)S(1)} all-to-all(bf16[8,2,128,128]{3,2,1,0:T(8,128)(2,1)} %bitcast.10), channel_id=1, replica_groups=mesh['row'=64,'col'=8] {'col'}, dimensions={0} | all-to-all | bytes 1048576 | tf_op jit(solution)/shard_map/all_to_all | solution.py:158
  552.1 0.1 convert_reduce_fusion
  552.1 1.0 convolution_convert_fusion
  553.1 0.1 broadcast_in_dim.3
  553.2 12.8 %all_to_all.38 = bf16[8,2,128,128]{3,2,1,0:T(8,128)(2,1)S(1)} all-to-all(bf16[8,2,128,128]{3,2,1,0:T(8,128)(2,1)S(1)} %broadcast_in_dim.3), channel_id=1, replica_groups=mesh['row'=64,'col'=8] {'col'}, dimensions={0} | all-to-all | bytes 1048576 | tf_op jit(solution)/shard_map/all_to_all | solution.py:165
  566.0 0.8 copy.15
Async XLA Ops:
  6.5 1.0 copy-start
  6.5 155.5 %all-gather.4.cloned.1.call-start = ((), (), s32[]{:S(2)}) async-start(), calls=%async_computation.6 | async-start | bytes 4259840 | tf_op jit(solution)/shard_map/all_gather | solution.py:147
  8.6 6.5 %collective-permute-start = (bf16[2,128,128]{2,1,0:T(8,128)(2,1)S(1)}, bf16[2,128,128]{2,1,0:T(8,128)(2,1)S(1)}, u32[]{:S(2)}, u32[]{:S(2)}) collective-permute-start(bf16[2,128,128]{2,1,0:T(8,128)(2,1)S(1)} %convolution_convert_fusion.3), channel_id=1, source_target_pairs={{0,0},{1,8},{2,16},{3,24},{4,32},{5,40},{6,48},{7,56},{8,1},{9,9},... | collective-permute-start | bytes 196616 | tf_op jit(solution)/shard_map/ppermute | solution.py:146
  15.1 0.6 copy-start.1
  40.8 53.9 %all-to-all-start.1 = ((bf16[8,16,128,128]{3,2,1,0:T(8,128)(2,1)}), bf16[8,16,128,128]{3,2,1,0:T(8,128)(2,1)}, u32[]{:S(2)}, u32[]{:S(2)}) async-start(bf16[8,16,128,128]{3,2,1,0:T(8,128)(2,1)} %bitcast.8), calls=%async_computation.1 | async-start | bytes 8388608 | tf_op jit(solution)/shard_map/all_to_all | solution.py:129
  45.9 293.6 %all-gather.6.cloned.1.call-start = ((), (), s32[]{:S(2)}) async-start(), calls=%async_computation.7 | async-start | bytes 4259840 | tf_op jit(solution)/shard_map/all_gather | solution.py:147
  198.2 6.1 %collective-permute-start.1 = (bf16[2,128,128]{2,1,0:T(8,128)(2,1)S(1)}, bf16[2,128,128]{2,1,0:T(8,128)(2,1)S(1)}, u32[]{:S(2)}, u32[]{:S(2)}) collective-permute-start(bf16[2,128,128]{2,1,0:T(8,128)(2,1)S(1)} %convolution_convert_fusion.2), channel_id=1, source_target_pairs={{0,0},{1,8},{2,16},{3,24},{4,32},{5,40},{6,48},{7,56},{8,1},{9,9},... | collective-permute-start | bytes 196616 | tf_op jit(solution)/shard_map/ppermute | solution.py:146
  204.3 0.6 copy-start.2
  204.9 312.0 %all-gather.8.cloned.1.call-start = ((), (), s32[]{:S(2)}) async-start(), calls=%async_computation.8 | async-start | bytes 4259840 | tf_op jit(solution)/shard_map/all_gather | solution.py:147
  375.7 6.1 %collective-permute-start.2 = (bf16[2,128,128]{2,1,0:T(8,128)(2,1)S(1)}, bf16[2,128,128]{2,1,0:T(8,128)(2,1)S(1)}, u32[]{:S(2)}, u32[]{:S(2)}) collective-permute-start(bf16[2,128,128]{2,1,0:T(8,128)(2,1)S(1)} %convolution_convert_fusion.1), channel_id=1, source_target_pairs={{0,0},{1,8},{2,16},{3,24},{4,32},{5,40},{6,48},{7,56},{8,1},{9,9},... | collective-permute-start | bytes 196616 | tf_op jit(solution)/shard_map/ppermute | solution.py:146
  381.8 0.6 copy-start.3
Sparse Core Ops, SparseCore 0:
  15.9 146.1 all-gather.3
  205.1 134.3 all-gather.5
  382.5 134.3 all-gather.7

commit v2 on v0

v2 whole, which is shorter than its diff:
```python
import jax
import jax.numpy as jnp
from jax import lax
from jax.experimental import pallas as pl
from jax.experimental.pallas import tpu as pltpu
from jax.sharding import PartitionSpec as P

ITERS = 4
CAP = 2
Y_SIZE = 4
MESH = pl.DeviceIdType.MESH


def place_kernel(rows, per_group, cols, room, owners, local, counts, blocks, placed, notes, live_at, dead_at, last, sem):
    slots = rows * per_group
    me = lax.axis_index("col")

    def clear(d, _):
        live_at[d] = 0
        dead_at[d] = room - 1
        last[d] = -1

        def blank(i, _):
            notes[d, 0, i] = 0
            return 0

        lax.fori_loop(0, 2 * room, blank, 0)

        def absent(i, _):
            notes[d, 0, 2 * room + i] = cols * room
            return 0

        lax.fori_loop(0, rows, absent, 0)
        return 0

    lax.fori_loop(0, cols, clear, 0)

    def one_row(row, _):
        count = counts[row]
        for k in range(per_group):
            owner = owners[row, k]
            group = owner // cols
            dest = owner - group * cols
            live = me + cols * k < count
            front = live_at[dest]
            back = dead_at[dest]
            at = jnp.where(live, front, back)

            @pl.when(live)
            def _():
                live_at[dest] = front + 1
                notes[dest, 0, at] = group * rows + local[row, k]
                notes[dest, 0, room + at] = (last[dest] == row).astype(jnp.int32)
                last[dest] = row
                notes[dest, 0, 2 * room + row] = me * room + at

            @pl.when(jnp.logical_not(live))
            def _():
                dead_at[dest] = back - 1

            pltpu.make_async_copy(blocks.at[row * per_group + k], placed.at[dest, at], sem).start()
        return 0

    lax.fori_loop(0, rows, one_row, 0)
    pltpu.make_async_copy(blocks, blocks, sem).wait()


def solve_kernel(
    rows, cols, row_count, room,
    placed, notes, inverse, right,
    out,
    blocks, noted, book, vec_0, vec_1, vec_2, mine, sums, part, got,
    block_send, block_recv, note_send, note_recv, book_sem,
    turn_send, turn_recv, ring_send, ring_recv, part_send, part_recv, last_send, last_recv,
):
    edge = inverse.shape[-1]
    share = rows // cols
    cut = edge * 5 // 8
    z_size = row_count // Y_SIZE
    row = lax.axis_index("row")
    col = lax.axis_index("col")
    z, y = row // Y_SIZE, lax.rem(row, Y_SIZE)
    group = row // cols
    within = row - group * cols
    partner_row, partner_col = group * cols + col, within
    straight = within == col

    def at(z_there, y_there):
        return lax.rem(z_there + z_size, z_size) * Y_SIZE + lax.rem(y_there + Y_SIZE, Y_SIZE)

    z_up, z_down, y_up, y_down = at(z + 1, y), at(z - 1, y), at(z, y + 1), at(z, y - 1)

    barrier = pltpu.get_barrier_semaphore()
    for d in range(1, cols):
        pl.semaphore_signal(barrier, inc=1, device_id=(row, lax.rem(col + d, cols)), device_id_type=MESH)
    for there in (z_up, z_down, y_up, y_down):
        pl.semaphore_signal(barrier, inc=1, device_id=(there, col), device_id_type=MESH)

    @pl.when(jnp.logical_not(straight))
    def _():
        pl.semaphore_signal(barrier, inc=1, device_id=(partner_row, partner_col), device_id_type=MESH)

    for b in range(share):
        mine[0, b] = jnp.dot(
            inverse[share * col + b], right[share * col + b], preferred_element_type=jnp.float32
        ).astype(jnp.bfloat16)
    sums[cols * room] = jnp.zeros(sums.shape[1:], jnp.float32)

    @pl.when(straight)
    def _():
        pl.semaphore_wait(barrier, cols + 3)

    @pl.when(jnp.logical_not(straight))
    def _():
        pl.semaphore_wait(barrier, cols + 4)

    def peers():
        return [lax.rem(col + d, cols) for d in range(1, cols)]

    for there in peers():
        pltpu.make_async_remote_copy(
            src_ref=notes.at[there], dst_ref=noted.at[col], send_sem=note_send, recv_sem=note_recv,
            device_id=(row, there), device_id_type=MESH,
        ).start()
    pltpu.make_async_copy(notes.at[col], noted.at[col], book_sem).start()
    pltpu.make_async_copy(placed.at[col], blocks.at[col], block_recv.at[col]).start()

    def send_blocks():
        for there in peers():
            pltpu.make_async_remote_copy(
                src_ref=placed.at[there], dst_ref=blocks.at[col], send_sem=block_send, recv_sem=block_recv.at[col],
                device_id=(row, there), device_id_type=MESH,
            ).start()

    vec = (vec_0, vec_1, vec_2)

    def whole(t, source):
        return vec[t].at[pl.ds(source * share, share)]

    def view(t, colour, source):
        span = pl.ds(0, cut) if colour == 0 else pl.ds(cut, edge - cut)
        return vec[t].at[pl.ds(source * share, share), span]

    def send(t, colour, source, there):
        pltpu.make_async_remote_copy(
            src_ref=view(t, colour, source), dst_ref=view(t, colour, source),
            send_sem=ring_send.at[t], recv_sem=ring_recv.at[t, colour, source],
            device_id=(there, col), device_id_type=MESH,
        ).start()

    def await_piece(t, colour, source):
        ref = view(t, colour, source)
        pltpu.make_async_copy(ref, ref, ring_recv.at[t, colour, source]).wait()

    half = z_size // 2
    reach = ((half, z_size - 1 - half), (z_size - 1 - half, half))

    def relay(t, colour, z_there):
        odd = lax.rem(z_there + z_size + y + 1, 2)
        source = jnp.where(odd == 0, at(z_there, y - 1), at(z_there, y + 1))
        send(t, colour, source, jnp.where(odd == 0, y_up, y_down))

    def pass_along_z(t, colour, y_there, k):
        up, down = reach[colour]
        fresh = []
        if k <= up:
            source = at(z - k, y_there)
            await_piece(t, colour, source)
            if k < up:
                send(t, colour, source, z_up)
            fresh.append(source)
        if k <= down:
            source = at(z + k, y_there)
            await_piece(t, colour, source)
            if k < down:
                send(t, colour, source, z_down)
            fresh.append(source)
        return fresh

    def gather(t):
        @pl.when(straight)
        def _():
            vec[t][pl.ds(row * share, share)] = mine[t]

        @pl.when(jnp.logical_not(straight))
        def _():
            copy = pltpu.make_async_remote_copy(
                src_ref=mine.at[t], dst_ref=whole(t, partner_row),
                send_sem=turn_send, recv_sem=turn_recv.at[t],
                device_id=(partner_row, partner_col), device_id_type=MESH,
            )
            copy.start()
            copy.wait_send()
            own = whole(t, row)
            pltpu.make_async_copy(own, own, turn_recv.at[t]).wait()

        send(t, 1, row, y_up)
        send(t, 1, row, y_down)
        send(t, 0, row, z_up)
        send(t, 0, row, z_down)
        send(t, 1, row, z_up)
        send(t, 1, row, z_down)
        send(t, 0, row, y_up)
        send(t, 0, row, y_down)

        if t == 0:
            send_blocks()

        for y_there in (y - 1, y + 1):
            source = at(z, y_there)
            await_piece(t, 1, source)
            send(t, 1, source, z_up)
            send(t, 1, source, z_down)
        relay(t, 1, z)
        late = []
        for k in range(1, half + 3):
            fresh = pass_along_z(t, 0, y, k)
            for source in fresh:
                send(t, 0, source, y_up)
                send(t, 0, source, y_down)
            for y_there in (y, y - 1, y + 1):
                pass_along_z(t, 1, y_there, k)
            if k == 1:
                source = at(z, y + 2)
                await_piece(t, 1, source)
                send(t, 1, source, z_up)
                send(t, 1, source, z_down)
            else:
                pass_along_z(t, 1, y + 2, k - 1)
            back = k - 1
            planes = []
            if back <= reach[0][0]:
                planes.append(z - back)
            if 0 < back <= reach[0][1]:
                planes.append(z + back)
            for z_there in planes:
                await_piece(t, 0, at(z_there, y - 1))
                await_piece(t, 0, at(z_there, y + 1))
                relay(t, 0, z_there)
                late.append(at(z_there, y + 2))
        for source in late:
            await_piece(t, 0, source)

    def products(t):
        def from_one(j, _):
            step = j // 2
            step = jnp.where(step == 2, cols // 2 - 1, jnp.where(step == 3, 2, step))
            across = lax.rem(j, 2)
            core = lax.rem(col, 2)
            source = lax.rem(col // 2 + step, cols // 2) * 2 + lax.rem(core + across, 2)

            if t == 0:
                ref = blocks.at[source]
                pltpu.make_async_copy(ref, ref, block_recv.at[source]).wait()

            total = None
            for p in range(room):
                column = book[source, 0, p]
                term = jnp.dot(
                    blocks[source, p],
                    vec[t][column],
                    preferred_element_type=jnp.float32,
                )
                if total is None:
                    total = term
                else:
                    total = total * book[source, 0, room + p].astype(jnp.float32) + term
                sums[source * room + p] = total
            return 0

        lax.fori_loop(0, cols, from_one, 0)

    def exchange(t):
        def to_one(j, _):
            there = lax.rem(col + 1 + j, cols)
            for b in range(share):
                r = share * there + b
                total = sums[book[0, 0, 2 * room + r]]
                for source in range(1, cols):
                    total = total + sums[book[source, 0, 2 * room + r]]
                part[t, there, b] = total.astype(jnp.bfloat16)

            @pl.when(j < cols - 1)
            def _():
                pltpu.make_async_remote_copy(
                    src_ref=part.at[t, there], dst_ref=got.at[t, col],
                    send_sem=part_send.at[t], recv_sem=part_recv.at[t],
                    device_id=(row, there), device_id_type=MESH,
                ).start()

            return 0

        lax.fori_loop(0, cols, to_one, 0)
        ref = got.at[t, pl.ds(0, cols - 1)]
        pltpu.make_async_copy(ref, ref, part_recv.at[t]).wait()
        got[t, col] = part[t, col]
        for b in range(share):
            total = got[t, 0, b].astype(jnp.float32)
            for source in range(1, cols):
                total = total + got[t, source, b].astype(jnp.float32)
            corrected = (right[share * col + b].astype(jnp.float32) - total).astype(jnp.bfloat16)
            mine[t + 1, b] = jnp.dot(
                inverse[share * col + b], corrected, preferred_element_type=jnp.float32
            ).astype(jnp.bfloat16)

    for t in range(ITERS - 1):
        gather(t)

        if t == 0:
            ref = noted.at[pl.ds(0, cols - 1)]
            pltpu.make_async_copy(ref, ref, note_recv).wait()
            pltpu.make_async_copy(notes.at[col], noted.at[col], book_sem).wait()
            copy = pltpu.make_async_copy(noted, book, book_sem)
            copy.start()
            copy.wait()

        products(t)
        exchange(t)

    for there in peers():
        pltpu.make_async_remote_copy(
            src_ref=mine.at[ITERS - 1], dst_ref=out.at[pl.ds(col * share, share)], send_sem=last_send, recv_sem=last_recv,
            device_id=(row, there), device_id_type=MESH,
        ).start()
    out[pl.ds(col * share, share)] = mine[ITERS - 1]
    ref = out.at[pl.ds(0, (cols - 1) * share)]
    pltpu.make_async_copy(ref, ref, last_recv).wait()

    pltpu.make_async_copy(ref, ref, last_send).wait()
    ref = blocks.at[pl.ds(0, cols - 1)]
    pltpu.make_async_copy(ref, ref, block_send).wait()
    ref = noted.at[pl.ds(0, cols - 1)]
    pltpu.make_async_copy(ref, ref, note_send).wait()
    for t in range(ITERS - 1):
        ref = got.at[t, pl.ds(0, cols - 1)]
        pltpu.make_async_copy(ref, ref, part_send.at[t]).wait()
        ref = vec[t].at[pl.ds(0, (row_count - 1) * share)]
        pltpu.make_async_copy(ref, ref, ring_send.at[t]).wait()


def shards(right_sides, inverse_diag, off_blocks, owners, local_block, counts):
    row_count = lax.axis_size("row")
    cols = lax.axis_size("col")
    rows = counts.shape[0]
    per_group = owners.shape[2]
    edge = off_blocks.shape[-1]
    width = right_sides.shape[-1]
    room = row_count // cols * CAP
    share = rows // cols
    rounds = ITERS - 1
    smem = pl.BlockSpec(memory_space=pltpu.SMEM)
    vmem = pl.BlockSpec(memory_space=pltpu.VMEM)
    anywhere = pl.BlockSpec(memory_space=pl.ANY)
    placed, notes = pl.pallas_call(
        lambda *refs: place_kernel(rows, per_group, cols, room, *refs),
        out_shape=(
            jax.ShapeDtypeStruct((cols, room, edge, edge), jnp.bfloat16),
            jax.ShapeDtypeStruct((cols, 1, 128), jnp.int32),
        ),
        in_specs=[smem, smem, smem, anywhere],
        out_specs=(vmem, smem),
        scratch_shapes=[pltpu.SMEM((cols,), jnp.int32)] * 3 + [pltpu.SemaphoreType.DMA],
    )(
        owners.reshape(rows, per_group),
        local_block.reshape(rows, per_group),
        counts,
        off_blocks.reshape(rows * per_group, edge, edge),
    )
    dma = pltpu.SemaphoreType.DMA
    return pl.pallas_call(
        lambda *refs: solve_kernel(rows, cols, row_count, room, *refs),
        out_shape=jax.ShapeDtypeStruct((rows, edge, width), jnp.bfloat16),
        in_specs=[anywhere, anywhere, vmem, vmem],
        out_specs=vmem,
        scratch_shapes=[
            pltpu.VMEM((cols, room, edge, edge), jnp.bfloat16),
            pltpu.VMEM((cols, 1, 128), jnp.int32),
            pltpu.SMEM((cols, 1, 128), jnp.int32),
            *[pltpu.VMEM((row_count * share, edge, width), jnp.bfloat16)] * rounds,
            pltpu.VMEM((rounds + 1, share, edge, width), jnp.bfloat16),
            pltpu.VMEM((cols * room + 1, edge, width), jnp.float32),
            pltpu.VMEM((rounds, cols, share, edge, width), jnp.bfloat16),
            pltpu.VMEM((rounds, cols, share, edge, width), jnp.bfloat16),
            dma,
            dma((cols,)),
            dma,
            dma,
            dma,
            dma,
            dma((rounds,)),
            dma((rounds,)),
            dma((rounds, 2, row_count)),
            dma((rounds,)),
            dma((rounds,)),
            dma,
            dma,
        ],
        compiler_params=pltpu.CompilerParams(
            collective_id=0, has_side_effects=True, vmem_limit_bytes=56 * 1024 * 1024
        ),
    )(placed, notes, inverse_diag, right_sides)


def solution(mesh):
    in_specs = (
        P("row", None, None),
        P("row", None, None),
        P("col", "row", None, None, None),
        P("col", "row", None),
        P("col", "row", None),
        P("row"),
    )
    out_specs = P("row", None, None)
    return jax.shard_map(shards, mesh=mesh, in_specs=in_specs, out_specs=out_specs, check_vma=False)
```

time: 746 us -> 206 us (0.28)
  blocking collectives: 455 us -> 0 us
  waiting for transfers between devices: 204 us -> 0 us
  Pallas kernels: 0 us -> 201 us
  starting transfers between devices: 37.8 us -> 0 us
  local copies, waits for them, and re-layouts: 29.2 us -> 4.59 us
  matrix products: 16.8 us -> 0 us
    all_to_all x7 -> x0, blocking collectives: 455 us -> none  [the longest x2 380 us: shards(): lax.all_to_all(outgoing, 'row', split_axis=0, concat_axis=0, tiled=True)]
    all_to_all x3 -> x0, waiting for transfers between devices: 204 us -> none  [the longest x1 182 us: shards(): lax.all_to_all(outgoing, 'row', split_axis=0, concat_axis=0, tiled=True)]
    pallas_call x0 -> x2, Pallas kernels: none -> 201 us  [the longest x1 193 us: shards(): pl.pallas_call(lambda *refs: solve_kernel(rows, cols, row_count, room, *r...]
    all_to_all x3 -> x0, starting transfers between devices: 37.8 us -> none  [the longest x1 19.3 us: shards(): lax.all_to_all(requests.reshape(row_count, capacity), 'row', split_axis=0...]
    gather x6 -> x0, local copies, waits for them, and re-layouts: 23.9 us -> none  [the longest x3 14.8 us: shards(): flattened[slot_place]]
    dot_general x7 -> x0, matrix products: 16.8 us -> none  [the longest x3 12.4 us: shards(): jnp.einsum('bkij,bkjr->bir', masked, picked, preferred_element_type=jnp.f...]
  transfers between devices with their start and end apart: 3 -> 0, of which waited for: 3 -> 0; matrix products, arithmetic and copies ran while one was open for 0% -> 0% of each run, Pallas kernels for 0% -> 0%
where the time goes in v2:
time: 206 us
  Pallas kernels  201 us (98%)
  local copies, waits for them, and re-layouts  4.59 us (2%)
    pallas_call x1, Pallas kernels, shards(): pl.pallas_call(lambda *refs: solve_kernel(rows, cols, row_count, room, *r...  193 us
    pallas_call x1, Pallas kernels, shards(): pl.pallas_call(lambda *refs: place_kernel(rows, per_group, cols, room, *r...  8.52 us

profile of v2, /device:TPU:1, one launch (start us, length us, event | category | flops | bytes accessed | tf_op | source)
XLA Modules:
  0.0 205.9 jit_solution(11765524813504496603)
XLA Ops:
  0.0 1.4 copy.9
  1.4 1.4 copy.10
  2.7 8.5 %shard_map.64 = (bf16[8,16,128,128]{3,2,1,0:T(8,128)(2,1)}, s32[8,1,128]{2,1,0:T(1,128)}) custom-call(s32[16,6]{1,0:T(8,128)} %bitcast.4, s32[16,6]{1,0:T(8,128)} %bitcast.5, s32[16]{0:T(128)} %refs_2_.2, bf16[96,128,128]{2,1,0:T(8,128)(2,1)} %bitcast.3), custom_call_target="tpu_custom_call" | custom-call | tf_op jit(solution)/shard_map/pallas_call | solution.py:354
  11.2 192.7 %shard_map.65 = bf16[16,128,128]{2,1,0:T(8,128)(2,1)} custom-call(bf16[8,16,128,128]{3,2,1,0:T(8,128)(2,1)} %get-tuple-element.7.refs_0_, s32[8,1,128]{2,1,0:T(1,128)} %get-tuple-element.8.refs_1_, bf16[16,128,128]{2,1,0:T(8,128)(2,1)} %refs_2_.3, bf16[16,128,128]{2,1,0:T(8,128)(2,1)} %refs_3_.1), custom_call_target="tpu_custom_call" | custom-call | tf_op jit(solution)/shard_map/pallas_call | solution.py:370
  204.0 1.9 copy.12

commit v3 on v2

--- a/solution.py
+++ b/solution.py
@@ -11,7 +11,7 @@
 MESH = pl.DeviceIdType.MESH
 
 
-def place_kernel(rows, per_group, cols, room, owners, local, counts, blocks, placed, notes, live_at, dead_at, last, sem):
+def place_kernel(rows, per_group, cols, room, share, owners, local, counts, blocks, placed, notes, live_at, dead_at, last, sem):
     slots = rows * per_group
     me = lax.axis_index("col")
 
@@ -20,17 +20,11 @@
         dead_at[d] = room - 1
         last[d] = -1
 
-        def blank(i, _):
+        for i in range(room):
             notes[d, 0, i] = 0
-            return 0
-
-        lax.fori_loop(0, 2 * room, blank, 0)
-
-        def absent(i, _):
+            notes[d, 0, room + i] = 0
+        for i in range(rows):
             notes[d, 0, 2 * room + i] = cols * room
-            return 0
-
-        lax.fori_loop(0, rows, absent, 0)
         return 0
 
     lax.fori_loop(0, cols, clear, 0)
@@ -38,7 +32,7 @@
     def one_row(row, _):
         count = counts[row]
         for k in range(per_group):
-            owner = owners[row, k]
+            owner = owners[k, 0, row]
             group = owner // cols
             dest = owner - group * cols
             live = me + cols * k < count
@@ -49,7 +43,8 @@
             @pl.when(live)
             def _():
                 live_at[dest] = front + 1
-                notes[dest, 0, at] = group * rows + local[row, k]
+                lane = local[k, 0, row]
+                notes[dest, 0, at] = group * rows + lane
                 notes[dest, 0, room + at] = (last[dest] == row).astype(jnp.int32)
                 last[dest] = row
                 notes[dest, 0, 2 * room + row] = me * room + at
@@ -71,29 +66,33 @@
     out,
     blocks, noted, book, vec_0, vec_1, vec_2, mine, sums, part, got,
     block_send, block_recv, note_send, note_recv, book_sem,
-    turn_send, turn_recv, ring_send, ring_recv, part_send, part_recv, last_send, last_recv,
+    give_send, give_recv, ring_send, ring_recv, part_send, part_recv, last_send, last_recv,
 ):
     edge = inverse.shape[-1]
     share = rows // cols
-    cut = edge * 5 // 8
+    cut = edge * 3 // 4
     z_size = row_count // Y_SIZE
     row = lax.axis_index("row")
     col = lax.axis_index("col")
     z, y = row // Y_SIZE, lax.rem(row, Y_SIZE)
     group = row // cols
     within = row - group * cols
+
+    def at(z_there, y_there):
+        return lax.rem(z_there + z_size, z_size) * Y_SIZE + lax.rem(y_there + Y_SIZE, Y_SIZE)
+
+    z_up, z_down, y_up, y_down = at(z + 1, y), at(z - 1, y), at(z, y + 1), at(z, y - 1)
+    z_up_2, z_down_2 = at(z + 2, y), at(z - 2, y)
+    spans = (pl.ds(0, cut // 2), pl.ds(cut // 2, cut // 2), pl.ds(cut, edge - cut))
+
     partner_row, partner_col = group * cols + col, within
     straight = within == col
-
-    def at(z_there, y_there):
-        return lax.rem(z_there + z_size, z_size) * Y_SIZE + lax.rem(y_there + Y_SIZE, Y_SIZE)
-
-    z_up, z_down, y_up, y_down = at(z + 1, y), at(z - 1, y), at(z, y + 1), at(z, y - 1)
 
     barrier = pltpu.get_barrier_semaphore()
     for d in range(1, cols):
         pl.semaphore_signal(barrier, inc=1, device_id=(row, lax.rem(col + d, cols)), device_id_type=MESH)
-    for there in (z_up, z_down, y_up, y_down):
+
+    for there in (z_up, z_down, z_up_2, z_down_2, y_up, y_down):
         pl.semaphore_signal(barrier, inc=1, device_id=(there, col), device_id_type=MESH)
 
     @pl.when(jnp.logical_not(straight))
@@ -106,26 +105,19 @@
         ).astype(jnp.bfloat16)
     sums[cols * room] = jnp.zeros(sums.shape[1:], jnp.float32)
 
-    @pl.when(straight)
-    def _():
-        pl.semaphore_wait(barrier, cols + 3)
-
-    @pl.when(jnp.logical_not(straight))
-    def _():
-        pl.semaphore_wait(barrier, cols + 4)
+    pl.semaphore_wait(barrier, cols + 5 + jnp.where(straight, 0, 1))
 
     def peers():
         return [lax.rem(col + d, cols) for d in range(1, cols)]
 
-    for there in peers():
-        pltpu.make_async_remote_copy(
-            src_ref=notes.at[there], dst_ref=noted.at[col], send_sem=note_send, recv_sem=note_recv,
-            device_id=(row, there), device_id_type=MESH,
-        ).start()
-    pltpu.make_async_copy(notes.at[col], noted.at[col], book_sem).start()
-    pltpu.make_async_copy(placed.at[col], blocks.at[col], block_recv.at[col]).start()
-
     def send_blocks():
+        for there in peers():
+            pltpu.make_async_remote_copy(
+                src_ref=notes.at[there], dst_ref=noted.at[col], send_sem=note_send, recv_sem=note_recv,
+                device_id=(row, there), device_id_type=MESH,
+            ).start()
+        pltpu.make_async_copy(notes.at[col], noted.at[col], book_sem).start()
+        pltpu.make_async_copy(placed.at[col], blocks.at[col], block_recv.at[col]).start()
         for there in peers():
             pltpu.make_async_remote_copy(
                 src_ref=placed.at[there], dst_ref=blocks.at[col], send_sem=block_send, recv_sem=block_recv.at[col],
@@ -134,50 +126,9 @@
 
     vec = (vec_0, vec_1, vec_2)
 
-    def whole(t, source):
-        return vec[t].at[pl.ds(source * share, share)]
-
-    def view(t, colour, source):
-        span = pl.ds(0, cut) if colour == 0 else pl.ds(cut, edge - cut)
-        return vec[t].at[pl.ds(source * share, share), span]
-
-    def send(t, colour, source, there):
-        pltpu.make_async_remote_copy(
-            src_ref=view(t, colour, source), dst_ref=view(t, colour, source),
-            send_sem=ring_send.at[t], recv_sem=ring_recv.at[t, colour, source],
-            device_id=(there, col), device_id_type=MESH,
-        ).start()
-
-    def await_piece(t, colour, source):
-        ref = view(t, colour, source)
-        pltpu.make_async_copy(ref, ref, ring_recv.at[t, colour, source]).wait()
-
-    half = z_size // 2
-    reach = ((half, z_size - 1 - half), (z_size - 1 - half, half))
-
-    def relay(t, colour, z_there):
-        odd = lax.rem(z_there + z_size + y + 1, 2)
-        source = jnp.where(odd == 0, at(z_there, y - 1), at(z_there, y + 1))
-        send(t, colour, source, jnp.where(odd == 0, y_up, y_down))
-
-    def pass_along_z(t, colour, y_there, k):
-        up, down = reach[colour]
-        fresh = []
-        if k <= up:
-            source = at(z - k, y_there)
-            await_piece(t, colour, source)
-            if k < up:
-                send(t, colour, source, z_up)
-            fresh.append(source)
-        if k <= down:
-            source = at(z + k, y_there)
-            await_piece(t, colour, source)
-            if k < down:
-                send(t, colour, source, z_down)
-            fresh.append(source)
-        return fresh
-
-    def gather(t):
+    def turn(t):
+        own = vec[t].at[pl.ds(row * share, share)]
+
         @pl.when(straight)
         def _():
             vec[t][pl.ds(row * share, share)] = mine[t]
@@ -185,61 +136,107 @@
         @pl.when(jnp.logical_not(straight))
         def _():
             copy = pltpu.make_async_remote_copy(
-                src_ref=mine.at[t], dst_ref=whole(t, partner_row),
-                send_sem=turn_send, recv_sem=turn_recv.at[t],
+                src_ref=mine.at[t], dst_ref=vec[t].at[pl.ds(partner_row * share, share)],
+                send_sem=give_send, recv_sem=give_recv.at[t],
                 device_id=(partner_row, partner_col), device_id_type=MESH,
             )
             copy.start()
             copy.wait_send()
-            own = whole(t, row)
-            pltpu.make_async_copy(own, own, turn_recv.at[t]).wait()
-
-        send(t, 1, row, y_up)
-        send(t, 1, row, y_down)
-        send(t, 0, row, z_up)
-        send(t, 0, row, z_down)
-        send(t, 1, row, z_up)
-        send(t, 1, row, z_down)
-        send(t, 0, row, y_up)
-        send(t, 0, row, y_down)
-
+            pltpu.make_async_copy(own, own, give_recv.at[t]).wait()
+
+    def view(t, colour, source):
+        return vec[t].at[pl.ds(source * share, share), spans[colour]]
+
+    def send(t, colour, source, there):
+        pltpu.make_async_remote_copy(
+            src_ref=view(t, colour, source), dst_ref=view(t, colour, source),
+            send_sem=ring_send.at[t, colour], recv_sem=ring_recv.at[t, colour, source],
+            device_id=(there, col), device_id_type=MESH,
+        ).start()
+
+    def await_piece(t, colour, source):
+        ref = view(t, colour, source)
+        pltpu.make_async_copy(ref, ref, ring_recv.at[t, colour, source]).wait()
+
+    half = z_size // 2
+    reach = ((half, half - 2), (half - 2, half), (half - 2, half))
+
+    def relay(t, colour, z_there):
+        odd = lax.rem(z_there + z_size + y + 1 + colour, 2)
+        source = jnp.where(odd == 0, at(z_there, y - 1), at(z_there, y + 1))
+        send(t, colour, source, jnp.where(odd == 0, y_up, y_down))
+
+    def onward(t, colour, source, k, ways=(0, 1)):
+        for way in ways:
+            if k < reach[colour][way]:
+                send(t, colour, source, (z_up_2, z_down_2)[way])
+            if k < half - 1:
+                send(t, colour, source, (z_up, z_down)[way])
+
+    def source_at(way, y_there, k):
+        return at(z + k if way else z - k, y_there)
+
+    def pass_along_z(t, colours, y_there, k):
+        fresh = []
+        for way in range(2):
+            source = source_at(way, y_there, k)
+            for colour in colours:
+                if k <= reach[colour][way]:
+                    await_piece(t, colour, source)
+                    onward(t, colour, source, k, (way,))
+                    fresh.append((colour, source, z + k if way else z - k))
+        return fresh
+
+    def ring(t):
+        send(t, 2, row, y_up)
+        send(t, 2, row, y_down)
+        for colour in (0, 1, 2):
+            onward(t, colour, row, 0)
+        for colour in (0, 1):
+            send(t, colour, row, y_up)
+            send(t, colour, row, y_down)
         if t == 0:
             send_blocks()
-
         for y_there in (y - 1, y + 1):
-            source = at(z, y_there)
-            await_piece(t, 1, source)
-            send(t, 1, source, z_up)
-            send(t, 1, source, z_down)
-        relay(t, 1, z)
+            await_piece(t, 2, at(z, y_there))
+            onward(t, 2, at(z, y_there), 0)
+        relay(t, 2, z)
         late = []
-        for k in range(1, half + 3):
-            fresh = pass_along_z(t, 0, y, k)
-            for source in fresh:
-                send(t, 0, source, y_up)
-                send(t, 0, source, y_down)
-            for y_there in (y, y - 1, y + 1):
-                pass_along_z(t, 1, y_there, k)
-            if k == 1:
-                source = at(z, y + 2)
-                await_piece(t, 1, source)
-                send(t, 1, source, z_up)
-                send(t, 1, source, z_down)
+        behind = [(0, z), (1, z)]
+        for k in range(2, half + 4, 2):
+            fresh = pass_along_z(t, (0, 1), y, k)
+            for way in range(2):
+                for colour in (0, 1):
+                    if k <= half:
+                        source = source_at(way, y, k - 1)
+                        await_piece(t, colour, source)
+                        fresh.append((colour, source, z + k - 1 if way else z - k + 1))
+            for colour, source, _ in fresh:
+                send(t, colour, source, y_up)
+                send(t, colour, source, y_down)
+            for y_there in (y, y + 1, y - 1):
+                pass_along_z(t, (2,), y_there, k)
+            if k == 2:
+                await_piece(t, 2, at(z, y + 2))
+                onward(t, 2, at(z, y + 2), 0)
             else:
-                pass_along_z(t, 1, y + 2, k - 1)
-            back = k - 1
-            planes = []
-            if back <= reach[0][0]:
-                planes.append(z - back)
-            if 0 < back <= reach[0][1]:
-                planes.append(z + back)
-            for z_there in planes:
-                await_piece(t, 0, at(z_there, y - 1))
-                await_piece(t, 0, at(z_there, y + 1))
-                relay(t, 0, z_there)
-                late.append(at(z_there, y + 2))
-        for source in late:
-            await_piece(t, 0, source)
+                pass_along_z(t, (2,), y + 2, k - 2)
+            for colour, z_there in behind:
+                await_piece(t, colour, at(z_there, y - 1))
+                await_piece(t, colour, at(z_there, y + 1))
+                relay(t, colour, z_there)
+                late.append((colour, at(z_there, y + 2)))
+            behind = [(colour, z_there) for colour, _, z_there in fresh]
+        for k in range(1, half, 2):
+            for y_there in (y, y + 1, y - 1, y + 2):
+                for way in range(2):
+                    await_piece(t, 2, source_at(way, y_there, k))
+        for colour, source in late:
+            await_piece(t, colour, source)
+
+    def gather(t):
+        turn(t)
+        ring(t)
 
     def products(t):
         def from_one(j, _):
@@ -334,8 +331,11 @@
     for t in range(ITERS - 1):
         ref = got.at[t, pl.ds(0, cols - 1)]
         pltpu.make_async_copy(ref, ref, part_send.at[t]).wait()
-        ref = vec[t].at[pl.ds(0, (row_count - 1) * share)]
-        pltpu.make_async_copy(ref, ref, ring_send.at[t]).wait()
+
+    for t in range(ITERS - 1):
+        for colour, span in enumerate(spans):
+            ref = vec[t].at[pl.ds(0, (row_count - 1) * share), span]
+            pltpu.make_async_copy(ref, ref, ring_send.at[t, colour]).wait()
 
 
 def shards(right_sides, inverse_diag, off_blocks, owners, local_block, counts):
@@ -352,7 +352,7 @@
     vmem = pl.BlockSpec(memory_space=pltpu.VMEM)
     anywhere = pl.BlockSpec(memory_space=pl.ANY)
     placed, notes = pl.pallas_call(
-        lambda *refs: place_kernel(rows, per_group, cols, room, *refs),
+        lambda *refs: place_kernel(rows, per_group, cols, room, share, *refs),
         out_shape=(
             jax.ShapeDtypeStruct((cols, room, edge, edge), jnp.bfloat16),
             jax.ShapeDtypeStruct((cols, 1, 128), jnp.int32),
@@ -361,8 +361,8 @@
         out_specs=(vmem, smem),
         scratch_shapes=[pltpu.SMEM((cols,), jnp.int32)] * 3 + [pltpu.SemaphoreType.DMA],
     )(
-        owners.reshape(rows, per_group),
-        local_block.reshape(rows, per_group),
+        owners.transpose(2, 0, 1),
+        local_block.transpose(2, 0, 1),
         counts,
         off_blocks.reshape(rows * per_group, edge, edge),
     )
@@ -388,8 +388,8 @@
             dma,
             dma,
             dma((rounds,)),
-            dma((rounds,)),
-            dma((rounds, 2, row_count)),
+            dma((rounds, 3)),
+            dma((rounds, 3, row_count)),
             dma((rounds,)),
             dma((rounds,)),
             dma,

time: 206 us -> 199 us (0.966)
  Pallas kernels: 201 us -> 197 us
  local copies, waits for them, and re-layouts: 4.59 us -> 1.89 us
    reshape x2 -> x0, local copies, waits for them, and re-layouts: 2.71 us -> none  [the longest x1 1.36 us: shards(): owners.reshape(rows, per_group)]
    pallas_call x1, Pallas kernels: 8.52 us -> 6.05 us  [shards(): pl.pallas_call(lambda *refs: place_kernel(rows, per_group, cols, room, sh...]
    pallas_call x1, Pallas kernels: 193 us -> 190 us  [shards(): pl.pallas_call(lambda *refs: solve_kernel(rows, cols, row_count, room, *r...]
where the time goes in v3:
time: 199 us; the launch traced here: 198 us
  Pallas kernels  197 us (99%)
    pallas_call x1, Pallas kernels, shards(): pl.pallas_call(lambda *refs: solve_kernel(rows, cols, row_count, room, *r...  190 us
    pallas_call x1, Pallas kernels, shards(): pl.pallas_call(lambda *refs: place_kernel(rows, per_group, cols, room, sh...  6.05 us

profile of v3, /device:TPU:1, one launch (start us, length us, event | category | flops | bytes accessed | tf_op | source)
XLA Modules:
  0.0 198.4 jit_solution(7965675581723508559)
XLA Ops:
  0.0 6.1 %shard_map.64 = (bf16[8,16,128,128]{3,2,1,0:T(8,128)(2,1)}, s32[8,1,128]{2,1,0:T(1,128)}) custom-call(s32[6,1,16]{2,1,0:T(1,128)} %bitcast.4, s32[6,1,16]{2,1,0:T(1,128)} %bitcast.5, s32[16]{0:T(128)} %refs_2_.2, bf16[96,128,128]{2,1,0:T(8,128)(2,1)} %bitcast.3), custom_call_target="tpu_custom_call" | custom-call | tf_op jit(solution)/shard_map/pallas_call | solution.py:354
  6.1 190.5 %shard_map.65 = bf16[16,128,128]{2,1,0:T(8,128)(2,1)} custom-call(bf16[8,16,128,128]{3,2,1,0:T(8,128)(2,1)} %get-tuple-element.7.refs_0_, s32[8,1,128]{2,1,0:T(1,128)} %get-tuple-element.8.refs_1_, bf16[16,128,128]{2,1,0:T(8,128)(2,1)} %refs_2_.3, bf16[16,128,128]{2,1,0:T(8,128)(2,1)} %refs_3_.1), custom_call_target="tpu_custom_call" | custom-call | tf_op jit(solution)/shard_map/pallas_call | solution.py:370
  196.5 1.9 copy.8

commit v4 on v3

--- a/solution.py
+++ b/solution.py
@@ -128,6 +128,11 @@
 
     def turn(t):
         own = vec[t].at[pl.ds(row * share, share)]
+        copy = pltpu.make_async_remote_copy(
+            src_ref=mine.at[t], dst_ref=vec[t].at[pl.ds(partner_row * share, share)],
+            send_sem=give_send, recv_sem=give_recv.at[t],
+            device_id=(partner_row, partner_col), device_id_type=MESH,
+        )
 
         @pl.when(straight)
         def _():
@@ -135,12 +140,13 @@
 
         @pl.when(jnp.logical_not(straight))
         def _():
-            copy = pltpu.make_async_remote_copy(
-                src_ref=mine.at[t], dst_ref=vec[t].at[pl.ds(partner_row * share, share)],
-                send_sem=give_send, recv_sem=give_recv.at[t],
-                device_id=(partner_row, partner_col), device_id_type=MESH,
-            )
             copy.start()
+
+        if t == 0:
+            send_blocks()
+
+        @pl.when(jnp.logical_not(straight))
+        def _():
             copy.wait_send()
             pltpu.make_async_copy(own, own, give_recv.at[t]).wait()
 
@@ -195,8 +201,6 @@
         for colour in (0, 1):
             send(t, colour, row, y_up)
             send(t, colour, row, y_down)
-        if t == 0:
-            send_blocks()
         for y_there in (y - 1, y + 1):
             await_piece(t, 2, at(z, y_there))
             onward(t, 2, at(z, y_there), 0)

time: 199 us -> 195 us (0.980)
  Pallas kernels: 197 us -> 192 us
    pallas_call x1, Pallas kernels: 190 us -> 186 us  [shards(): pl.pallas_call(lambda *refs: solve_kernel(rows, cols, row_count, room, *r...]
where the time goes in v4:
time: 195 us; the launch traced here: 194 us
  Pallas kernels  192 us (98%)
    pallas_call x1, Pallas kernels, shards(): pl.pallas_call(lambda *refs: solve_kernel(rows, cols, row_count, room, *r...  186 us
    pallas_call x1, Pallas kernels, shards(): pl.pallas_call(lambda *refs: place_kernel(rows, per_group, cols, room, sh...  6.05 us

profile of v4, /device:TPU:1, one launch (start us, length us, event | category | flops | bytes accessed | tf_op | source)
XLA Modules:
  0.0 194.3 jit_solution(11851311066374021241)
XLA Ops:
  0.0 6.1 %shard_map.64 = (bf16[8,16,128,128]{3,2,1,0:T(8,128)(2,1)}, s32[8,1,128]{2,1,0:T(1,128)}) custom-call(s32[6,1,16]{2,1,0:T(1,128)} %bitcast.4, s32[6,1,16]{2,1,0:T(1,128)} %bitcast.5, s32[16]{0:T(128)} %refs_2_.2, bf16[96,128,128]{2,1,0:T(8,128)(2,1)} %bitcast.3), custom_call_target="tpu_custom_call" | custom-call | tf_op jit(solution)/shard_map/pallas_call | solution.py:358
  6.1 186.4 %shard_map.65 = bf16[16,128,128]{2,1,0:T(8,128)(2,1)} custom-call(bf16[8,16,128,128]{3,2,1,0:T(8,128)(2,1)} %get-tuple-element.7.refs_0_, s32[8,1,128]{2,1,0:T(1,128)} %get-tuple-element.8.refs_1_, bf16[16,128,128]{2,1,0:T(8,128)(2,1)} %refs_2_.3, bf16[16,128,128]{2,1,0:T(8,128)(2,1)} %refs_3_.1), custom_call_target="tpu_custom_call" | custom-call | tf_op jit(solution)/shard_map/pallas_call | solution.py:374
  192.4 1.9 copy.8
